TPU v7x, 32 devices: a whole 2x2x4 slice. The times are simulated.
32 devices in a mesh: row: 4 (over z), col: 8 (over y, x, core).
Axes of the slice: x: 2, y: 2, z: 4, core: 2. Of those that a mesh axis runs over, the one named last changes fastest.
Arguments:
- green: float32 [512, 16384], P(('row', 'col')), may hold values from -0.375 to 0.375
- noise_precision: float32 [512], P(('row', 'col')), may hold values from 0.5 to 4
- data_set: int32 [512], P(('row', 'col')), may hold values from 0 to 3
- set_scale: float32 [4], replicated, may hold values from 0.5 to 2
- stiffness: float32 [8192], replicated, may hold values from 0.25 to 2
- patch_cell: int32 [8192], replicated, may hold values from 0 to 8191, each once
Outputs:
- precision_matrix: float32 [16384, 16384], P('row', 'col')
Inputs may be any that keep to these rules, and one draw needn't show every extreme that they name: `patch_cell`: every cell 0 to 8191 holds exactly one patch.
All inputs are finite; a program needn't handle non-finite values.
Results may differ from a plain program's by a relative error of at most 0.00005.
Values sent between devices are 32-bit elements; how exact they have to be, the bound alone decides.
A program may use at most 256 MiB of HBM per device.

v0:
```python
import jax
import jax.numpy as jnp
from jax import lax
from jax.experimental import pallas as pl
from jax.experimental.pallas import tpu as pltpu
from jax.sharding import PartitionSpec as P

NSTRIKE = 128
NDIP = 64


def gram_product(left_panel, right_panel):
    return lax.dot_general(
        left_panel,
        right_panel,
        (((0,), (0,)), ((), ())),
        precision=lax.Precision.HIGH,
        preferred_element_type=jnp.float32,
    )


def one_hots(cells):
    strike_hot = cells[:, None] // NDIP == jnp.arange(NSTRIKE, dtype=jnp.int32)[None, :]
    dip_hot = cells[:, None] % NDIP == jnp.arange(NDIP, dtype=jnp.int32)[None, :]
    return strike_hot, dip_hot


def degree_table(stiffness, patch_cell):
    strike_hot, dip_hot = one_hots(patch_cell)
    grid = lax.dot_general(
        strike_hot.astype(jnp.float32),
        jnp.where(dip_hot, stiffness[:, None], 0.0),
        (((0,), (0,)), ((), ())),
        precision=lax.Precision.HIGHEST,
        preferred_element_type=jnp.float32,
    )
    padded = jnp.pad(grid, 1)
    strike_ids = lax.broadcasted_iota(jnp.int32, (NSTRIKE, NDIP), 0)
    dip_ids = lax.broadcasted_iota(jnp.int32, (NSTRIKE, NDIP), 1)
    degree = jnp.zeros((NSTRIKE, NDIP), jnp.float32)
    degree = degree + jnp.where(strike_ids < NSTRIKE - 1, 0.5 * (grid + padded[2:, 1:-1]), 0.0)
    degree = degree + jnp.where(strike_ids > 0, 0.5 * (grid + padded[:-2, 1:-1]), 0.0)
    degree = degree + jnp.where(dip_ids < NDIP - 1, 0.5 * (grid + padded[1:-1, 2:]), 0.0)
    degree = degree + jnp.where(dip_ids > 0, 0.5 * (grid + padded[1:-1, :-2]), 0.0)
    return degree


def degree_of(degree, cells):
    strike_hot, dip_hot = one_hots(cells)
    lines = jnp.dot(
        strike_hot.astype(jnp.float32),
        degree,
        precision=lax.Precision.HIGHEST,
        preferred_element_type=jnp.float32,
    )
    return jnp.sum(jnp.where(dip_hot, lines, 0.0), axis=1)


def smoothing_tile(stiffness, patch_cell, row_start, tile_height, col_start, tile_width):
    patch_count = stiffness.shape[0]
    degree_cells = degree_table(stiffness, patch_cell)
    row_first = row_start % patch_count
    col_first = col_start % patch_count
    row_cell = lax.dynamic_slice_in_dim(patch_cell, row_first, tile_height, 0)
    col_cell = lax.dynamic_slice_in_dim(patch_cell, col_first, tile_width, 0)
    row_stiff = lax.dynamic_slice_in_dim(stiffness, row_first, tile_height, 0)
    col_stiff = lax.dynamic_slice_in_dim(stiffness, col_first, tile_width, 0)
    row_degree = degree_of(degree_cells, row_cell)
    row_strike = row_cell // NDIP
    row_dip = row_cell % NDIP
    col_strike = col_cell // NDIP
    col_dip = col_cell % NDIP
    spacing = jnp.abs(row_strike[:, None] - col_strike[None, :]) + jnp.abs(
        row_dip[:, None] - col_dip[None, :]
    )
    row_ids = row_start + jnp.arange(tile_height, dtype=jnp.int32)
    col_ids = col_start + jnp.arange(tile_width, dtype=jnp.int32)
    same_part = row_ids[:, None] // patch_count == col_ids[None, :] // patch_count
    coupling = jnp.where(
        (spacing == 1) & same_part, -0.5 * (row_stiff[:, None] + col_stiff[None, :]), 0.0
    )
    diagonal = row_ids[:, None] == col_ids[None, :]
    return coupling + jnp.where(diagonal, row_degree[:, None], 0.0)


def exchange_kernel(row_count, col_count, block, by_row, by_column, send, recv, own):
    row = lax.axis_index("row")
    col = lax.axis_index("col")
    rows = block.shape[0]
    height = by_row.shape[1]
    width = by_column.shape[1]
    row_slot = by_row.at[pl.ds(pl.multiple_of(row * rows, 8), rows), :]
    col_slot = by_column.at[pl.ds(pl.multiple_of(col * rows, 8), rows), :]
    copies = []
    for step in range(1, row_count):
        target = lax.rem(row + step, row_count)
        copies.append(
            pltpu.make_async_remote_copy(
                src_ref=block.at[:, pl.ds(pl.multiple_of(target * height, 128), height)],
                dst_ref=row_slot,
                send_sem=send.at[step - 1],
                recv_sem=recv.at[step - 1],
                device_id=(target, col),
                device_id_type=pl.DeviceIdType.MESH,
            )
        )
    for step in range(1, col_count):
        target = lax.rem(col + step, col_count)
        copies.append(
            pltpu.make_async_remote_copy(
                src_ref=block.at[:, pl.ds(pl.multiple_of(target * width, 128), width)],
                dst_ref=col_slot,
                send_sem=send.at[row_count + step - 2],
                recv_sem=recv.at[row_count + step - 2],
                device_id=(row, target),
                device_id_type=pl.DeviceIdType.MESH,
            )
        )
    copies.append(
        pltpu.make_async_copy(
            block.at[:, pl.ds(pl.multiple_of(row * height, 128), height)], row_slot, own.at[0]
        )
    )
    copies.append(
        pltpu.make_async_copy(
            block.at[:, pl.ds(pl.multiple_of(col * width, 128), width)], col_slot, own.at[1]
        )
    )
    for copy in copies:
        copy.start()
    for copy in copies:
        copy.wait()


def exchange(scaled, row_count, col_count):
    rows, order_full = scaled.shape
    in_vmem = pl.BlockSpec(memory_space=pltpu.VMEM)
    partners = row_count + col_count - 2

    def body(*refs):
        exchange_kernel(row_count, col_count, *refs)

    return pl.pallas_call(
        body,
        out_shape=(
            jax.ShapeDtypeStruct((row_count * rows, order_full // row_count), jnp.float32),
            jax.ShapeDtypeStruct((col_count * rows, order_full // col_count), jnp.float32),
        ),
        in_specs=[in_vmem],
        out_specs=(in_vmem, in_vmem),
        scratch_shapes=[
            pltpu.SemaphoreType.DMA((partners,)),
            pltpu.SemaphoreType.DMA((partners,)),
            pltpu.SemaphoreType.DMA((2,)),
        ],
        compiler_params=pltpu.CompilerParams(has_side_effects=True),
    )(scaled)


def per_device(green, noise_precision, data_set, set_scale, stiffness, patch_cell):
    row_count = lax.axis_size("row")
    col_count = lax.axis_size("col")
    local_rows = green.shape[0]
    order_full = green.shape[1]
    tile_height = order_full // row_count
    tile_width = order_full // col_count
    matches = data_set[:, None] == jnp.arange(set_scale.shape[0], dtype=jnp.int32)[None, :]
    weight = noise_precision * jnp.sum(jnp.where(matches, set_scale[None, :], 0.0), axis=1)
    scaled = green * jnp.sqrt(weight)[:, None]
    by_row, by_column = exchange(scaled, row_count, col_count)
    right_factor = lax.all_gather(by_column, "row", axis=0, tiled=True)
    reordered = jnp.transpose(
        right_factor.reshape(row_count, col_count, local_rows, tile_width), (1, 0, 2, 3)
    ).reshape(row_count * col_count * local_rows, tile_width)
    gram_tile = gram_product(lax.all_gather(by_row, "col", axis=0, tiled=True), reordered)
    prior = smoothing_tile(
        stiffness,
        patch_cell,
        lax.axis_index("row") * tile_height,
        tile_height,
        lax.axis_index("col") * tile_width,
        tile_width,
    )
    return gram_tile + prior


def solution(mesh):
    placed = (P(("row", "col"), None), P(("row", "col")), P(("row", "col")), P(), P(), P())
    return jax.shard_map(
        per_device, mesh=mesh, in_specs=placed, out_specs=P("row", "col"), check_vma=False
    )
```

profile of v0, /device:TPU:16, one launch (start us, length us, event | category | flops | bytes accessed | tf_op | source)
XLA Modules:
  0.0 237.9 jit_solution(9080004859607463196)
XLA Ops:
  6.5 0.0 all-gather.5.cloned.1.call-start
  6.5 0.8 select_reduce_fusion
  7.3 0.7 multiply_sqrt_fusion
  8.0 2.3 broadcast_multiply_fusion.refs_0_
  10.3 31.7 %shard_map.64 = (f32[64,4096]{1,0:T(8,128)}, f32[128,2048]{1,0:T(8,128)}) custom-call(f32[16,16384]{1,0:T(8,128)} %broadcast_multiply_fusion.refs_0_), custom_call_target="tpu_custom_call" | custom-call | tf_op jit(solution)/shard_map/pallas_call | solution.py:143
  42.0 0.0 all-gather.5.cloned.1.call-update
  42.0 0.0 all-gather.3.cloned.1.call-start
  42.0 0.7 all-gather.3.cloned.1.call-update
  42.8 0.7 dynamic_slice.15
  43.5 0.7 dynamic_slice.14
  44.2 0.7 add_select_fusion.7
  45.0 0.7 add_select_fusion.3
  45.7 0.7 add_select_fusion.4
  46.5 0.8 add_select_fusion
  47.2 2.7 %fusion.1 = f32[128,64]{0,1:T(8,128)S(1)} fusion(s32[8192]{0:T(1024)S(1)} %get-tuple-element.14, f32[8192]{0:T(1024)} %param.10, s32[8192]{0:T(1024)S(1)} %get-tuple-element.13), kind=kOutput, calls=%fused_computation.5 | convolution fusion | flops 807403520 | bytes 131072 | tf_op jit(solution)/shard_map/dot_general | solution.py:30
  50.0 1.6 fusion.4
  51.6 0.7 add_select_fusion.6
  52.3 70.9 %all-gather.5.cloned.1.call-done = f32[512,2048]{1,0:T(8,128)} async-done(((f32[128,2048]{1,0:T(8,128)}), f32[512,2048]{1,0:T(8,128)}) %all-gather.5.cloned.1.call-update) | async-done | bytes 4194320 | tf_op jit(solution)/shard_map/all_gather | solution.py:171
  123.2 4.6 %copy.8 = f32[4,8,16,2048]{3,2,0,1:T(8,128)} copy(f32[4,8,16,2048]{3,2,1,0:T(8,128)} %bitcast.6) | data formatting | bytes 8388608 | tf_op jit(solution)/shard_map/reshape | solution.py:173
  127.9 51.5 %all-gather.3.cloned.1.call-done = f32[512,4096]{1,0:T(8,128)} async-done(((f32[64,4096]{1,0:T(8,128)}), f32[512,4096]{1,0:T(8,128)}) %all-gather.3.cloned.1.call-update) | async-done | bytes 8388624 | tf_op jit(solution)/shard_map/all_gather | solution.py:175
  179.4 51.7 %add_add_fusion = f32[4096,2048]{1,0:T(8,128)} fusion(f32[4096]{0:T(1024)S(1)} %fusion.4, s32[2048]{0:T(1024)S(1)} %get-tuple-element.22, f32[2048]{0:T(1024)S(1)} %dynamic_slice.15, f32[4096]{0:T(1024)S(1)} %dynamic_slice.14, s32[2048]{0:T(1024)S(1)} %get-tuple-element.21, s32[2048]{0:T(1024)S(1)} %add_select_fusion.6, s32[4096]{0:T(1024)S(1)} %get-tuple-element.11, ...), kind=kOutput, calls=%fused_computation | convolution fusion | flops 25895632896 | bytes 46276608 | tf_op jit(solution)/shard_map/dot_general | solution.py:13
  (4 shorter events, 0.0 us)
Async XLA Ops:
  6.5 116.7 %all-gather.5.cloned.1.call-start = ((), (), s32[]{:S(2)}) async-start(), calls=%async_computation.1 | async-start | bytes 5242880 | tf_op jit(solution)/shard_map/all_gather | solution.py:171
  42.0 137.4 %all-gather.3.cloned.1.call-start = ((), (), s32[]{:S(2)}) async-start(), calls=%async_computation | async-start | bytes 9437184 | tf_op jit(solution)/shard_map/all_gather | solution.py:175
Sparse Core Ops, SparseCore 0:
  42.1 81.0 all-gather.4
  125.1 54.2 all-gather.2
where the time goes:
time: 240 us; the launch traced here: 238 us
  waiting for transfers between devices  123 us (51%)
  matrix products  56 us (23%)
  Pallas kernels  31.7 us (13%)
  between operations  13.5 us (6%)
  other arithmetic  7.48 us (3%)
  local copies, waits for them, and re-layouts  6.04 us (3%)
    all_gather x1, waiting for transfers between devices, per_device(): right_factor = lax.all_gather(by_column, 'row', axis=0, tiled=True)  70.9 us
    dot_general x1, matrix products, gram_product(): lax.dot_general(left_panel, right_panel, (((0,), (0,)), ((), ())), precis...  51.7 us
    all_gather x1, waiting for transfers between devices, per_device(): lax.all_gather(by_row, 'col', axis=0, tiled=True)  51.5 us
    pallas_call x1, Pallas kernels, exchange(): pl.pallas_call(body, out_shape=(jax.ShapeDtypeStruct((row_count * rows, o...  31.7 us
  transfers between devices with their start and end apart: 2, of which 2 were waited for; matrix products, arithmetic and copies ran while one was open for 6% of the time, Pallas kernels for 0%

commit v1 on v0

v1 whole, which is shorter than its diff:
```python
import jax
import jax.numpy as jnp
from jax import lax
from jax.experimental import pallas as pl
from jax.experimental.pallas import tpu as pltpu
from jax.sharding import PartitionSpec as P

NSTRIKE = 128
NDIP = 64
LANES = 128
VMEM_GRANT = 16 * 2**20
MESH = pl.DeviceIdType.MESH


def xor(value, other, count):
    total = 0
    bit = 1
    while bit < count:
        total = total + ((value // bit) % 2 + (other // bit) % 2) % 2 * bit
        bit *= 2
    return total


def ring_chip(place, chips):
    return jnp.where(place < chips // 2, place, chips + chips // 2 - 1 - place)


def plane_at(row, order, row_count):
    low = jnp.where(order % 2 == 1, row - (order + 1) // 2, row + order // 2)
    near = jnp.minimum(row, row_count - 1 - row)
    far = jnp.where(row < row_count - 1 - row, order, row_count - 1 - order)
    return jnp.where(order <= 2 * near, low, far)


def split_two(values):
    high = values.astype(jnp.bfloat16)
    low = (values - high.astype(jnp.float32)).astype(jnp.bfloat16)
    return high, low


def split_three(values):
    high = values.astype(jnp.bfloat16)
    rest = values - high.astype(jnp.float32)
    middle = rest.astype(jnp.bfloat16)
    low = (rest - middle.astype(jnp.float32)).astype(jnp.bfloat16)
    return high, middle, low


def contract_rows(left, right):
    return lax.dot_general(left, right, (((0,), (0,)), ((), ())), preferred_element_type=jnp.float32)


def load_right(col, plane, right):
    depth = col.shape[1]
    high, low = split_two(col[plane])
    right[pl.ds(0, depth), :] = high
    right[pl.ds(depth, depth), :] = high
    right[pl.ds(2 * depth, depth), :] = low


def strip_left(rowp, plane, start, height):
    width = rowp.shape[3]
    half = start // width
    first = pl.multiple_of(start % width, LANES)
    high, low = split_two(rowp[half, plane, :, pl.ds(first, height)])
    return jnp.concatenate([high, low, high], axis=0)


def code_of(cells):
    return ((cells // NDIP) * (2 * NDIP) + cells % NDIP).astype(jnp.float32)


def hot_strike(cells):
    ids = lax.broadcasted_iota(jnp.int32, (NSTRIKE, LANES), 0)
    return jnp.where(ids == cells // NDIP, 1.0, 0.0)


def hot_dip(cells):
    ids = lax.broadcasted_iota(jnp.int32, (LANES, LANES), 0)
    return ids == cells % NDIP


def degree_grid(stiff, cell):
    lines = cell.shape[0]

    def add(step, total):
        strike = hot_strike(cell[pl.ds(step, 1), :]).astype(jnp.bfloat16)
        hot = hot_dip(cell[pl.ds(step, 1), :])
        parts = split_three(jnp.where(hot, stiff[pl.ds(step, 1), :], 0.0))
        return total + lax.dot_general(
            strike,
            jnp.concatenate(parts, axis=0),
            (((1,), (1,)), ((), ())),
            preferred_element_type=jnp.float32,
        )

    sums = lax.fori_loop(0, lines, add, jnp.zeros((NSTRIKE, 3 * LANES), jnp.float32))
    grid = sums[:, :LANES] + sums[:, LANES : 2 * LANES] + sums[:, 2 * LANES :]
    strike_ids = lax.broadcasted_iota(jnp.int32, (NSTRIKE, LANES), 0)
    dip_ids = lax.broadcasted_iota(jnp.int32, (NSTRIKE, LANES), 1)
    degree = jnp.where(strike_ids < NSTRIKE - 1, 0.5 * (grid + pltpu.roll(grid, NSTRIKE - 1, 0)), 0.0)
    degree = degree + jnp.where(strike_ids > 0, 0.5 * (grid + pltpu.roll(grid, 1, 0)), 0.0)
    degree = degree + jnp.where(dip_ids < NDIP - 1, 0.5 * (grid + pltpu.roll(grid, LANES - 1, 1)), 0.0)
    degree = degree + jnp.where(dip_ids > 0, 0.5 * (grid + pltpu.roll(grid, 1, 1)), 0.0)
    return degree


def degree_line(parts, cells):
    strike = hot_strike(cells).astype(jnp.bfloat16)
    table = contract_rows(parts[0], strike) + contract_rows(parts[1], strike) + contract_rows(parts[2], strike)
    return jnp.sum(jnp.where(hot_dip(cells), table, 0.0), axis=0, keepdims=True)


def prior_strip(stiff, cell, acc, row_line, col_line, start, height, same):
    width = acc.shape[1]

    @pl.when(same)
    def _():
        @pl.loop(0, height // LANES)
        def _(block):
            first = pl.multiple_of(start + block * LANES, LANES)
            line = row_line + first // LANES
            full = (LANES, LANES)
            row_code = jnp.broadcast_to(code_of(cell[pl.ds(line, 1), :]), full).T
            row_half = jnp.broadcast_to(-0.5 * stiff[pl.ds(line, 1), :], full).T
            for place in range(width // LANES):
                other = col_line + place
                apart = jnp.abs(row_code - code_of(cell[pl.ds(other, 1), :]))
                edge = row_half - 0.5 * stiff[pl.ds(other, 1), :]
                near = (apart == 1.0) | (apart == 2.0 * NDIP)
                acc[pl.ds(first, LANES), pl.ds(place * LANES, LANES)] = jnp.where(near, edge, 0.0)

    @pl.when(jnp.logical_not(same))
    def _():
        acc[pl.ds(start, height), :] = jnp.zeros((height, width), jnp.float32)


def gather_kernel(
    row_count,
    col_count,
    green,
    noise,
    data_set,
    set_scale,
    stiff,
    cell,
    acc,
    rowp,
    col,
    scaled,
    right,
    send_plane,
    recv_plane,
    send_up,
    send_down,
    recv_z,
    send_cw,
    send_ccw,
    recv_ring,
    send_core,
    recv_core,
):
    row = lax.axis_index("row")
    me = lax.axis_index("col")
    core = me % 2
    chip = me // 2
    chips = col_count // 2
    rows, order_full = green.shape
    height, width = acc.shape
    patches = stiff.shape[0] * LANES
    owner = chip == row
    home = 2 * row + core
    partner = 2 * chip + 1 - core
    place = ring_chip(chip, chips)
    hop_cw = lax.rem(place - ring_chip(row, chips) + chips, chips)
    hop_ccw = lax.rem(chips - hop_cw, chips)
    next_cw = 2 * ring_chip(lax.rem(place + 1, chips), chips) + core
    next_ccw = 2 * ring_chip(lax.rem(place + chips - 1, chips), chips) + core
    has_up = row + 1 < row_count
    has_down = row > 0
    above = jnp.minimum(row + 1, row_count - 1)
    below = jnp.maximum(row - 1, 0)

    barrier = pltpu.get_barrier_semaphore()
    for step in range(1, col_count):
        pl.semaphore_signal(barrier, inc=1, device_id=(row, xor(me, step, col_count)), device_id_type=MESH)

    @pl.when(has_up)
    def _():
        pl.semaphore_signal(barrier, inc=1, device_id=(above, me), device_id_type=MESH)

    @pl.when(has_down)
    def _():
        pl.semaphore_signal(barrier, inc=1, device_id=(below, me), device_id_type=MESH)

    row_ids = lax.broadcasted_iota(jnp.int32, (rows, LANES), 0)
    weight = jnp.zeros((rows, LANES), jnp.float32)
    for entry in range(rows):
        weight = jnp.where(row_ids == entry, noise[entry] * set_scale[data_set[entry]], weight)
    factor = jnp.sqrt(weight)

    @pl.loop(0, order_full // LANES)
    def _(step):
        lanes = pl.ds(pl.multiple_of(step * LANES, LANES), LANES)
        scaled[:, lanes] = green[:, lanes] * factor

    def slab(index):
        return pl.ds(pl.multiple_of(index * rows, rows), rows)

    own = pl.ds(pl.multiple_of(me * width, LANES), width)
    col[row, slab(me), :] = scaled[:, own]
    pl.semaphore_wait(barrier, col_count - 1 + has_up.astype(jnp.int32) + has_down.astype(jnp.int32))

    def plane_copy(step):
        target = xor(me, step, col_count)
        return pltpu.make_async_remote_copy(
            src_ref=scaled.at[:, pl.ds(pl.multiple_of(target * width, LANES), width)],
            dst_ref=col.at[row, slab(me), :],
            send_sem=send_plane.at[step],
            recv_sem=recv_plane.at[step],
            device_id=(row, target),
            device_id_type=MESH,
        )

    for step in range(1, col_count):
        plane_copy(step).start()

    def z_copy(plane, step, up):
        where = slab(xor(me, step, col_count))
        return pltpu.make_async_remote_copy(
            src_ref=col.at[plane, where, :],
            dst_ref=col.at[plane, where, :],
            send_sem=send_up.at[plane] if up else send_down.at[plane],
            recv_sem=recv_z.at[plane, step],
            device_id=(above if up else below, me),
            device_id_type=MESH,
        )

    def ring_copy(plane, step, clockwise, source):
        where = slab(xor(home, step, col_count))
        return pltpu.make_async_remote_copy(
            src_ref=source.at[plane, where, :],
            dst_ref=rowp.at[core, plane, where, :],
            send_sem=send_cw.at[plane] if clockwise else send_ccw.at[plane],
            recv_sem=recv_ring.at[plane, step],
            device_id=(row, next_cw if clockwise else next_ccw),
            device_id_type=MESH,
        )

    def core_copy(plane, step, source):
        where = slab(xor(home, step, col_count))
        return pltpu.make_async_remote_copy(
            src_ref=source.at[plane, where, :],
            dst_ref=rowp.at[core, plane, where, :],
            send_sem=send_core.at[plane],
            recv_sem=recv_core.at[plane],
            device_id=(row, partner),
            device_id_type=MESH,
        )

    def arrived(plane, step):
        @pl.when(has_up & (plane <= row))
        def _():
            z_copy(plane, step, True).start()

        @pl.when(has_down & (plane >= row))
        def _():
            z_copy(plane, step, False).start()

        @pl.when(owner)
        def _():
            @pl.when(step % 2 == 0)
            def _():
                ring_copy(plane, step, True, col).start()

            @pl.when(step % 2 == 1)
            def _():
                ring_copy(plane, step, False, col).start()

            core_copy(plane, step, col).start()
            where = slab(xor(home, step, col_count))
            rowp[core, plane, where, :] = col[plane, where, :]

    held = rowp.at[core]

    def ring_step(plane, step, hop, clockwise):
        ring_copy(plane, step, clockwise, held).wait_recv()

        @pl.when(hop < chips - 1)
        def _():
            ring_copy(plane, step, clockwise, held).start()

        core_copy(plane, step, held).start()

    def both_sides(distance, act):
        @pl.when(row - distance >= 0)
        def _():
            act(row - distance)

        @pl.when((distance > 0) & (row + distance < row_count))
        def _():
            act(row + distance)

    def wait_core(plane):
        whole = rowp.at[1 - core, plane]
        pltpu.make_async_remote_copy(
            src_ref=whole,
            dst_ref=whole,
            send_sem=send_core.at[plane],
            recv_sem=recv_core.at[plane],
            device_id=(row, partner),
            device_id_type=MESH,
        ).wait_recv()

    lag = 2 * (chips - 1)
    steps = row_count * col_count
    strip = height // col_count
    same = (row * height) // patches == (me * width) // patches
    row_line = lax.rem(row * height, patches) // LANES
    col_line = lax.rem(me * width, patches) // LANES

    @pl.loop(0, steps + lag)
    def _(now):
        distance = now // col_count
        step = lax.rem(now, col_count)

        @pl.when((now > 0) & (now < col_count))
        def _():
            pltpu.make_async_remote_copy(
                src_ref=col.at[row, slab(xor(me, step, col_count)), :],
                dst_ref=col.at[row, slab(xor(me, step, col_count)), :],
                send_sem=send_plane.at[step],
                recv_sem=recv_plane.at[step],
                device_id=(row, partner),
                device_id_type=MESH,
            ).wait_recv()

        @pl.when(now < steps)
        def _():
            def receive(plane):
                @pl.when(now >= col_count)
                def _():
                    z_copy(plane, step, True).wait_recv()

                arrived(plane, step)

            both_sides(distance, receive)

        def ring_turn(hop, clockwise):
            late = now - 2 * hop

            @pl.when((hop > 0) & (late >= 0) & (late < steps))
            def _():
                both_sides(
                    late // col_count,
                    lambda plane: ring_step(plane, lax.rem(late, col_count), hop, clockwise),
                )

        @pl.when(now % 2 == 0)
        def _():
            ring_turn(hop_cw, True)

        @pl.when(now % 2 == 1)
        def _():
            ring_turn(hop_ccw, False)

        @pl.when(now < col_count)
        def _():
            prior_strip(stiff, cell, acc, row_line, col_line, pl.multiple_of(step * strip, LANES), strip, same)

        @pl.when((now == col_count) & owner)
        def _():
            parts = split_three(degree_grid(stiff, cell))
            corner = lax.broadcasted_iota(jnp.int32, (LANES, LANES), 0) == lax.broadcasted_iota(
                jnp.int32, (LANES, LANES), 1
            )

            @pl.loop(0, width // LANES)
            def _(block):
                line = degree_line(parts, cell[pl.ds(col_line + block, 1), :])
                across = pl.ds(pl.multiple_of(block * LANES, LANES), LANES)
                down = pl.ds(pl.multiple_of(core * width + block * LANES, LANES), LANES)
                acc[down, across] = acc[down, across] + jnp.where(corner, line, 0.0)

        turn = now - col_count - lag

        @pl.when(turn >= 0)
        def _():
            plane = plane_at(row, turn // col_count, row_count)
            part = lax.rem(turn, col_count)

            @pl.when(part == 0)
            def _():
                wait_core(plane)
                load_right(col, plane, right)

            start = pl.multiple_of(part * strip, LANES)
            left = strip_left(rowp, plane, start, strip)
            piece = min(width, 512)

            @pl.loop(0, width // piece)
            def _(block):
                across = pl.ds(pl.multiple_of(block * piece, LANES), piece)
                down = pl.ds(start, strip)
                acc[down, across] = acc[down, across] + contract_rows(left, right[:, across])

    wait_core(plane_at(row, row_count - 1, row_count))

    for step in range(1, col_count):
        plane_copy(step).wait_send()

    @pl.loop(0, row_count)
    def _(plane):
        whole = col.at[plane]
        half = whole.at[pl.ds(0, whole.shape[0] // 2), :]

        def sent(ref, sem):
            pltpu.make_async_remote_copy(
                src_ref=ref,
                dst_ref=ref,
                send_sem=sem,
                recv_sem=recv_core.at[plane],
                device_id=(row, partner),
                device_id_type=MESH,
            ).wait_send()

        sent(whole, send_core.at[plane])

        @pl.when(has_up & (plane <= row))
        def _():
            sent(whole, send_up.at[plane])

        @pl.when(has_down & (plane >= row))
        def _():
            sent(whole, send_down.at[plane])

        @pl.when(hop_cw < chips - 1)
        def _():
            sent(half, send_cw.at[plane])

        @pl.when(hop_ccw < chips - 1)
        def _():
            sent(half, send_ccw.at[plane])


def gather_and_sum(row_count, col_count, green, noise, data_set, set_scale, stiff, cell):
    rows, order_full = green.shape
    height = order_full // row_count
    width = order_full // col_count
    depth = col_count * rows
    vmem = pl.BlockSpec(memory_space=pltpu.VMEM)
    smem = pl.BlockSpec(memory_space=pltpu.SMEM)
    dma = pltpu.SemaphoreType.DMA

    def body(*refs):
        gather_kernel(row_count, col_count, *refs)

    return pl.pallas_call(
        body,
        out_shape=(
            pltpu.VMEM((height, width), jnp.float32),
            pltpu.VMEM((2, row_count, depth, width), jnp.float32),
            pltpu.VMEM((row_count, depth, width), jnp.float32),
        ),
        in_specs=[vmem, smem, smem, smem, vmem, vmem],
        out_specs=(vmem, vmem, vmem),
        scratch_shapes=[
            pltpu.VMEM((rows, order_full), jnp.float32),
            pltpu.VMEM((3 * depth, width), jnp.bfloat16),
            dma((col_count,)),
            dma((col_count,)),
            dma((row_count,)),
            dma((row_count,)),
            dma((row_count, col_count)),
            dma((row_count,)),
            dma((row_count,)),
            dma((row_count, col_count)),
            dma((row_count,)),
            dma((row_count,)),
        ],
        compiler_params=pltpu.CompilerParams(
            collective_id=0, has_side_effects=True, vmem_limit_bytes=VMEM_GRANT
        ),
    )(green, noise, data_set, set_scale, stiff, cell)


def finish_kernel(row_count, slots, acc, rowp, col, out, stage, right, sems):
    row = lax.axis_index("row")
    plane = plane_at(row, row_count - 1, row_count)
    height, width = acc.shape
    strip = stage.shape[1]
    piece = min(width, 512)
    load_right(col, plane, right)

    def copy(index, slot):
        start = pl.multiple_of(index * strip, LANES)
        return pltpu.make_async_copy(stage.at[slot], out.at[pl.ds(start, strip), :], sems.at[slot])

    count = height // strip

    @pl.loop(0, count)
    def _(index):
        slot = lax.rem(index, slots)

        @pl.when(index >= slots)
        def _():
            copy(index - slots, slot).wait()

        start = pl.multiple_of(index * strip, LANES)
        left = strip_left(rowp, plane, start, strip)

        @pl.loop(0, width // piece)
        def _(block):
            across = pl.ds(pl.multiple_of(block * piece, LANES), piece)
            stage[slot, :, across] = acc[pl.ds(start, strip), across] + contract_rows(left, right[:, across])

        copy(index, slot).start()

    for back in range(slots):
        index = count - slots + back
        copy(index, index % slots).wait()


def finish(row_count, acc, rowp, col):
    height, width = acc.shape
    depth = col.shape[1]
    vmem = pl.BlockSpec(memory_space=pltpu.VMEM)
    strip = min(height, 256)
    slots = 4

    def body(*refs):
        finish_kernel(row_count, slots, *refs)

    return pl.pallas_call(
        body,
        out_shape=jax.ShapeDtypeStruct((height, width), jnp.float32),
        in_specs=[vmem, vmem, vmem],
        out_specs=pl.BlockSpec(memory_space=pl.ANY),
        scratch_shapes=[
            pltpu.VMEM((slots, strip, width), jnp.float32),
            pltpu.VMEM((3 * depth, width), jnp.bfloat16),
            pltpu.SemaphoreType.DMA((slots,)),
        ],
        compiler_params=pltpu.CompilerParams(vmem_limit_bytes=VMEM_GRANT),
    )(*(pltpu.with_memory_space_constraint(array, pltpu.VMEM) for array in (acc, rowp, col)))


def per_device(green, noise_precision, data_set, set_scale, stiffness, patch_cell):
    row_count = lax.axis_size("row")
    col_count = lax.axis_size("col")
    lines = stiffness.shape[0] // LANES
    acc, rowp, col = gather_and_sum(
        row_count,
        col_count,
        green,
        noise_precision,
        data_set,
        set_scale,
        stiffness.reshape(lines, LANES),
        patch_cell.reshape(lines, LANES),
    )
    return finish(row_count, acc, rowp, col)


def solution(mesh):
    placed = (P(("row", "col"), None), P(("row", "col")), P(("row", "col")), P(), P(), P())
    return jax.shard_map(
        per_device, mesh=mesh, in_specs=placed, out_specs=P("row", "col"), check_vma=False
    )
```

time: 240 us -> 131 us (0.55)
  waiting for transfers between devices: 123 us -> 0 us
  Pallas kernels: 31.7 us -> 131 us
  matrix products: 56 us -> 0 us
  between operations: 13.5 us -> 0.01 us
  other arithmetic: 7.48 us -> 0 us
  local copies, waits for them, and re-layouts: 6.04 us -> 0 us
    all_gather x2 -> x0, waiting for transfers between devices: 122 us -> none  [the longest x1 70.9 us: per_device(): right_factor = lax.all_gather(by_column, 'row', axis=0, tiled=True)]
    pallas_call x1 -> x2, Pallas kernels: 31.7 us -> 131 us  [the longest x1 108 us: gather_and_sum(): pl.pallas_call(body, out_shape=(pltpu.VMEM((height, width), jnp.float32),...]
    dot_general x3 -> x0, matrix products: 56 us -> none  [the longest x1 51.7 us: gram_product(): lax.dot_general(left_panel, right_panel, (((0,), (0,)), ((), ())), precis...]
    reshape x1 -> x0, local copies, waits for them, and re-layouts: 4.62 us -> none  [per_device(): right_factor.reshape(row_count, col_count, local_rows, tile_width)]
    select_n x7 -> x0, other arithmetic: 3.72 us -> none  [the longest x1 0.79 us: one_hots(): cells[:, None] % NDIP == jnp.arange(NDIP, dtype=jnp.int32)[None, :]]
  transfers between devices with their start and end apart: 2 -> 0, of which waited for: 2 -> 0; matrix products, arithmetic and copies ran while one was open for 6% -> 0% of each run, Pallas kernels for 0% -> 0%
where the time goes in v1:
time: 131 us
  Pallas kernels  131 us (100%)
    pallas_call x1, Pallas kernels, gather_and_sum(): pl.pallas_call(body, out_shape=(pltpu.VMEM((height, width), jnp.float32),...  108 us
    pallas_call x1, Pallas kernels, finish(): pl.pallas_call(body, out_shape=jax.ShapeDtypeStruct((height, width), jnp....  22.7 us

profile of v1, /device:TPU:16, one launch (start us, length us, event | category | flops | bytes accessed | tf_op | source)
XLA Modules:
  0.0 130.6 jit_solution(11440770208551910750)
XLA Ops:
  0.0 107.9 %shard_map.64 = (f32[4096,2048]{1,0:T(8,128)S(1)}, f32[2,4,128,2048]{3,2,1,0:T(8,128)S(1)}, f32[4,128,2048]{2,1,0:T(8,128)S(1)}) custom-call(f32[16,16384]{1,0:T(8,128)} %refs_0_.1, f32[16]{0:T(128)} %refs_1_.1, s32[16]{0:T(128)} %refs_2_.1, f32[4]{0:T(128)} %refs_3_.1, f32[64,128]{1,0:T(8,128)} %bitcast.2, s32[64,128]{1,0:T(8,128)} %bitcast.3), custom_call_target="tpu_custom_call" | custom-call | tf_op jit(solution)/shard_map/pallas_call | solution.py:458
  107.9 22.7 %shard_map.65 = f32[4096,2048]{1,0:T(8,128)} custom-call(f32[4096,2048]{1,0:T(8,128)S(1)} %get-tuple-element.8.refs_0_, f32[2,4,128,2048]{3,2,1,0:T(8,128)S(1)} %get-tuple-element.9.refs_1_, f32[4,128,2048]{2,1,0:T(8,128)S(1)} %get-tuple-element.10.refs_2_), custom_call_target="tpu_custom_call" | custom-call | tf_op jit(solution)/shard_map/pallas_call | solution.py:534

commit v2 on v1

--- a/solution.py
+++ b/solution.py
@@ -394,15 +394,13 @@
                 wait_core(plane)
                 load_right(col, plane, right)
 
-            start = pl.multiple_of(part * strip, LANES)
-            left = strip_left(rowp, plane, start, strip)
-            piece = min(width, 512)
-
-            @pl.loop(0, width // piece)
+            piece = min(strip, 2 * LANES)
+
+            @pl.loop(0, strip // piece)
             def _(block):
-                across = pl.ds(pl.multiple_of(block * piece, LANES), piece)
-                down = pl.ds(start, strip)
-                acc[down, across] = acc[down, across] + contract_rows(left, right[:, across])
+                start = pl.multiple_of(part * strip + block * piece, LANES)
+                left = strip_left(rowp, plane, start, piece)
+                acc[pl.ds(start, piece), :] = acc[pl.ds(start, piece), :] + contract_rows(left, right[...])
 
     wait_core(plane_at(row, row_count - 1, row_count))
 
@@ -489,7 +487,6 @@
     plane = plane_at(row, row_count - 1, row_count)
     height, width = acc.shape
     strip = stage.shape[1]
-    piece = min(width, 512)
     load_right(col, plane, right)
 
     def copy(index, slot):
@@ -509,11 +506,7 @@
         start = pl.multiple_of(index * strip, LANES)
         left = strip_left(rowp, plane, start, strip)
 
-        @pl.loop(0, width // piece)
-        def _(block):
-            across = pl.ds(pl.multiple_of(block * piece, LANES), piece)
-            stage[slot, :, across] = acc[pl.ds(start, strip), across] + contract_rows(left, right[:, across])
-
+        stage[slot] = acc[pl.ds(start, strip), :] + contract_rows(left, right[...])
         copy(index, slot).start()
 
     for back in range(slots):

time: 131 us -> 115 us (0.88)
  Pallas kernels: 131 us -> 115 us
    pallas_call x1, Pallas kernels: 22.7 us -> 13.4 us  [finish(): pl.pallas_call(body, out_shape=jax.ShapeDtypeStruct((height, width), jnp....]
    pallas_call x1, Pallas kernels: 108 us -> 101 us  [gather_and_sum(): pl.pallas_call(body, out_shape=(pltpu.VMEM((height, width), jnp.float32),...]
where the time goes in v2:
time: 115 us
  Pallas kernels  115 us (100%)
    pallas_call x1, Pallas kernels, gather_and_sum(): pl.pallas_call(body, out_shape=(pltpu.VMEM((height, width), jnp.float32),...  101 us
    pallas_call x1, Pallas kernels, finish(): pl.pallas_call(body, out_shape=jax.ShapeDtypeStruct((height, width), jnp....  13.4 us

profile of v2, /device:TPU:16, one launch (start us, length us, event | category | flops | bytes accessed | tf_op | source)
XLA Modules:
  0.0 114.6 jit_solution(18234330333627837787)
XLA Ops:
  0.0 101.2 %shard_map.64 = (f32[4096,2048]{1,0:T(8,128)S(1)}, f32[2,4,128,2048]{3,2,1,0:T(8,128)S(1)}, f32[4,128,2048]{2,1,0:T(8,128)S(1)}) custom-call(f32[16,16384]{1,0:T(8,128)} %refs_0_.1, f32[16]{0:T(128)} %refs_1_.1, s32[16]{0:T(128)} %refs_2_.1, f32[4]{0:T(128)} %refs_3_.1, f32[64,128]{1,0:T(8,128)} %bitcast.2, s32[64,128]{1,0:T(8,128)} %bitcast.3), custom_call_target="tpu_custom_call" | custom-call | tf_op jit(solution)/shard_map/pallas_call | solution.py:456
  101.2 13.4 %shard_map.65 = f32[4096,2048]{1,0:T(8,128)} custom-call(f32[4096,2048]{1,0:T(8,128)S(1)} %get-tuple-element.8.refs_0_, f32[2,4,128,2048]{3,2,1,0:T(8,128)S(1)} %get-tuple-element.9.refs_1_, f32[4,128,2048]{2,1,0:T(8,128)S(1)} %get-tuple-element.10.refs_2_), custom_call_target="tpu_custom_call" | custom-call | tf_op jit(solution)/shard_map/pallas_call | solution.py:527

commit v3 on v2

--- a/solution.py
+++ b/solution.py
@@ -8,7 +8,7 @@
 NSTRIKE = 128
 NDIP = 64
 LANES = 128
-VMEM_GRANT = 16 * 2**20
+VMEM_GRANT = 19 * 2**20
 MESH = pl.DeviceIdType.MESH
 
 
@@ -50,20 +50,23 @@
     return lax.dot_general(left, right, (((0,), (0,)), ((), ())), preferred_element_type=jnp.float32)
 
 
-def load_right(col, plane, right):
+def load_right(col, planes, right):
     depth = col.shape[1]
-    high, low = split_two(col[plane])
-    right[pl.ds(0, depth), :] = high
-    right[pl.ds(depth, depth), :] = high
-    right[pl.ds(2 * depth, depth), :] = low
-
-
-def strip_left(rowp, plane, start, height):
+    for index, plane in enumerate(planes):
+        high, low = split_two(col[plane])
+        for part, values in enumerate((high, high, low)):
+            right[pl.ds((3 * index + part) * depth, depth), :] = values
+
+
+def strip_left(rowp, planes, start, height):
     width = rowp.shape[3]
     half = start // width
     first = pl.multiple_of(start % width, LANES)
-    high, low = split_two(rowp[half, plane, :, pl.ds(first, height)])
-    return jnp.concatenate([high, low, high], axis=0)
+    parts = []
+    for plane in planes:
+        high, low = split_two(rowp[half, plane, :, pl.ds(first, height)])
+        parts += [high, low, high]
+    return jnp.concatenate(parts, axis=0)
 
 
 def code_of(cells):
@@ -81,20 +84,26 @@
 
 
 def degree_grid(stiff, cell):
-    lines = cell.shape[0]
+    group = 8
 
     def add(step, total):
-        strike = hot_strike(cell[pl.ds(step, 1), :]).astype(jnp.bfloat16)
-        hot = hot_dip(cell[pl.ds(step, 1), :])
-        parts = split_three(jnp.where(hot, stiff[pl.ds(step, 1), :], 0.0))
+        strikes = []
+        parts = ([], [], [])
+        for inner in range(group):
+            cells = cell[pl.ds(step * group + inner, 1), :]
+            strikes.append(hot_strike(cells).astype(jnp.bfloat16))
+            chosen = jnp.where(hot_dip(cells), stiff[pl.ds(step * group + inner, 1), :], 0.0)
+            for part, values in zip(parts, split_three(chosen)):
+                part.append(values)
+        tables = jnp.concatenate([jnp.concatenate(part, axis=1) for part in parts], axis=0)
         return total + lax.dot_general(
-            strike,
-            jnp.concatenate(parts, axis=0),
+            jnp.concatenate(strikes, axis=1),
+            tables,
             (((1,), (1,)), ((), ())),
             preferred_element_type=jnp.float32,
         )
 
-    sums = lax.fori_loop(0, lines, add, jnp.zeros((NSTRIKE, 3 * LANES), jnp.float32))
+    sums = lax.fori_loop(0, cell.shape[0] // group, add, jnp.zeros((NSTRIKE, 3 * LANES), jnp.float32))
     grid = sums[:, :LANES] + sums[:, LANES : 2 * LANES] + sums[:, 2 * LANES :]
     strike_ids = lax.broadcasted_iota(jnp.int32, (NSTRIKE, LANES), 0)
     dip_ids = lax.broadcasted_iota(jnp.int32, (NSTRIKE, LANES), 1)
@@ -258,7 +267,12 @@
             device_id_type=MESH,
         )
 
-    def arrived(plane, step):
+    def reach(distance, step):
+        around = jnp.where(distance == row_count - 1, chips // 2, chips - 1)
+        beside = jnp.where(distance == row_count - 1, chips // 2 - 1, 0)
+        return jnp.where(step % 2 == 0, around, beside)
+
+    def arrived(plane, step, distance):
         @pl.when(has_up & (plane <= row))
         def _():
             z_copy(plane, step, True).start()
@@ -269,11 +283,13 @@
 
         @pl.when(owner)
         def _():
-            @pl.when(step % 2 == 0)
+            clockwise = reach(distance, step)
+
+            @pl.when(clockwise > 0)
             def _():
                 ring_copy(plane, step, True, col).start()
 
-            @pl.when(step % 2 == 1)
+            @pl.when(clockwise < chips - 1)
             def _():
                 ring_copy(plane, step, False, col).start()
 
@@ -283,10 +299,10 @@
 
     held = rowp.at[core]
 
-    def ring_step(plane, step, hop, clockwise):
+    def ring_step(plane, step, clockwise, onward):
         ring_copy(plane, step, clockwise, held).wait_recv()
 
-        @pl.when(hop < chips - 1)
+        @pl.when(onward)
         def _():
             ring_copy(plane, step, clockwise, held).start()
 
@@ -315,11 +331,13 @@
     lag = 2 * (chips - 1)
     steps = row_count * col_count
     strip = height // col_count
+    inner = has_up & has_down
+    behind = jnp.where(inner, 0, 0)
     same = (row * height) // patches == (me * width) // patches
     row_line = lax.rem(row * height, patches) // LANES
     col_line = lax.rem(me * width, patches) // LANES
 
-    @pl.loop(0, steps + lag)
+    @pl.loop(0, steps + lag + 2)
     def _(now):
         distance = now // col_count
         step = lax.rem(now, col_count)
@@ -342,33 +360,30 @@
                 def _():
                     z_copy(plane, step, True).wait_recv()
 
-                arrived(plane, step)
+                arrived(plane, step, distance)
 
             both_sides(distance, receive)
 
-        def ring_turn(hop, clockwise):
-            late = now - 2 * hop
-
-            @pl.when((hop > 0) & (late >= 0) & (late < steps))
+        def ring_turn(hop, clockwise, behind, first, last):
+            late = now - 2 * hop - behind
+            far = late // col_count
+            turn = lax.rem(late, col_count)
+            limit = reach(far, turn)
+            limit = limit if clockwise else chips - 1 - limit
+
+            @pl.when((hop > 0) & (late >= first) & (late < last) & (hop <= limit))
             def _():
-                both_sides(
-                    late // col_count,
-                    lambda plane: ring_step(plane, lax.rem(late, col_count), hop, clockwise),
-                )
-
-        @pl.when(now % 2 == 0)
-        def _():
-            ring_turn(hop_cw, True)
-
-        @pl.when(now % 2 == 1)
-        def _():
-            ring_turn(hop_ccw, False)
-
-        @pl.when(now < col_count)
+                both_sides(far, lambda plane: ring_step(plane, turn, clockwise, hop < limit))
+
+        for hop, clockwise in ((hop_cw, True), (hop_ccw, False)):
+            ring_turn(hop, clockwise, 0, 0, col_count)
+            ring_turn(hop, clockwise, behind, col_count, steps)
+
+        @pl.when((now >= col_count) & (now < 2 * col_count))
         def _():
             prior_strip(stiff, cell, acc, row_line, col_line, pl.multiple_of(step * strip, LANES), strip, same)
 
-        @pl.when((now == col_count) & owner)
+        @pl.when((now == 2 * col_count) & owner)
         def _():
             parts = split_three(degree_grid(stiff, cell))
             corner = lax.broadcasted_iota(jnp.int32, (LANES, LANES), 0) == lax.broadcasted_iota(
@@ -382,25 +397,35 @@
                 down = pl.ds(pl.multiple_of(core * width + block * LANES, LANES), LANES)
                 acc[down, across] = acc[down, across] + jnp.where(corner, line, 0.0)
 
-        turn = now - col_count - lag
-
-        @pl.when(turn >= 0)
-        def _():
-            plane = plane_at(row, turn // col_count, row_count)
-            part = lax.rem(turn, col_count)
-
-            @pl.when(part == 0)
+        def add_planes(begin, orders, strip):
+            part = now - begin
+
+            @pl.when((part >= 0) & (part * strip < height))
             def _():
-                wait_core(plane)
-                load_right(col, plane, right)
-
-            piece = min(strip, 2 * LANES)
-
-            @pl.loop(0, strip // piece)
-            def _(block):
-                start = pl.multiple_of(part * strip + block * piece, LANES)
-                left = strip_left(rowp, plane, start, piece)
-                acc[pl.ds(start, piece), :] = acc[pl.ds(start, piece), :] + contract_rows(left, right[...])
+                planes = [plane_at(row, order, row_count) for order in orders]
+
+                @pl.when(part == 0)
+                def _():
+                    for plane in planes:
+                        wait_core(plane)
+                    load_right(col, planes, right)
+
+                piece = min(strip, 4 * LANES)
+                used = right.at[pl.ds(0, 3 * len(planes) * col.shape[1]), :]
+
+                @pl.loop(0, strip // piece)
+                def _(block):
+                    start = pl.multiple_of(part * strip + block * piece, LANES)
+                    left = strip_left(rowp, planes, start, piece)
+                    acc[pl.ds(start, piece), :] = acc[pl.ds(start, piece), :] + contract_rows(left, used[...])
+
+        if row_count == 4:
+            first = jnp.where(inner, 1, 0)
+            add_planes(2 * col_count + lag + behind, (first, first + 1), strip)
+            add_planes(jnp.where(inner, 2 * col_count, 3 * col_count + lag), (jnp.where(inner, 0, 2),), 2 * strip)
+        else:
+            order = jnp.clip((now - lag - 2) // col_count - 1, 0, row_count - 2)
+            add_planes((order + 1) * col_count + lag + 2, (order,), strip)
 
     wait_core(plane_at(row, row_count - 1, row_count))
 
@@ -432,13 +457,16 @@
         def _():
             sent(whole, send_down.at[plane])
 
-        @pl.when(hop_cw < chips - 1)
-        def _():
-            sent(half, send_cw.at[plane])
-
-        @pl.when(hop_ccw < chips - 1)
-        def _():
-            sent(half, send_ccw.at[plane])
+        for step in range(2):
+            limit = reach(jnp.abs(plane - row), step)
+
+            @pl.when(hop_cw < limit)
+            def _():
+                sent(half, send_cw.at[plane])
+
+            @pl.when(hop_ccw < chips - 1 - limit)
+            def _():
+                sent(half, send_ccw.at[plane])
 
 
 def gather_and_sum(row_count, col_count, green, noise, data_set, set_scale, stiff, cell):
@@ -464,7 +492,7 @@
         out_specs=(vmem, vmem, vmem),
         scratch_shapes=[
             pltpu.VMEM((rows, order_full), jnp.float32),
-            pltpu.VMEM((3 * depth, width), jnp.bfloat16),
+            pltpu.VMEM((6 * depth, width), jnp.bfloat16),
             dma((col_count,)),
             dma((col_count,)),
             dma((row_count,)),
@@ -487,7 +515,7 @@
     plane = plane_at(row, row_count - 1, row_count)
     height, width = acc.shape
     strip = stage.shape[1]
-    load_right(col, plane, right)
+    load_right(col, (plane,), right)
 
     def copy(index, slot):
         start = pl.multiple_of(index * strip, LANES)
@@ -504,7 +532,7 @@
             copy(index - slots, slot).wait()
 
         start = pl.multiple_of(index * strip, LANES)
-        left = strip_left(rowp, plane, start, strip)
+        left = strip_left(rowp, (plane,), start, strip)
 
         stage[slot] = acc[pl.ds(start, strip), :] + contract_rows(left, right[...])
         copy(index, slot).start()
@@ -518,8 +546,8 @@
     height, width = acc.shape
     depth = col.shape[1]
     vmem = pl.BlockSpec(memory_space=pltpu.VMEM)
-    strip = min(height, 256)
-    slots = 4
+    strip = min(height, 512)
+    slots = 3
 
     def body(*refs):
         finish_kernel(row_count, slots, *refs)

time: 115 us -> 106 us (0.922)
  the two profiles are of different devices: /device:TPU:16 before, /device:TPU:25 now
where the time goes in v3:
time: 106 us
  Pallas kernels  106 us (100%)
    pallas_call x1, Pallas kernels, gather_and_sum(): pl.pallas_call(body, out_shape=(pltpu.VMEM((height, width), jnp.float32),...  93 us
    pallas_call x1, Pallas kernels, finish(): pl.pallas_call(body, out_shape=jax.ShapeDtypeStruct((height, width), jnp....  12.6 us

profile of v3, /device:TPU:25, one launch (start us, length us, event | category | flops | bytes accessed | tf_op | source)
XLA Modules:
  0.0 105.6 jit_solution(4646279547626728341)
XLA Ops:
  0.0 93.0 %shard_map.64 = (f32[4096,2048]{1,0:T(8,128)S(1)}, f32[2,4,128,2048]{3,2,1,0:T(8,128)S(1)}, f32[4,128,2048]{2,1,0:T(8,128)S(1)}) custom-call(f32[16,16384]{1,0:T(8,128)} %refs_0_.1, f32[16]{0:T(128)} %refs_1_.1, s32[16]{0:T(128)} %refs_2_.1, f32[4]{0:T(128)} %refs_3_.1, f32[64,128]{1,0:T(8,128)} %bitcast.2, s32[64,128]{1,0:T(8,128)} %bitcast.3), custom_call_target="tpu_custom_call" | custom-call | tf_op jit(solution)/shard_map/pallas_call | solution.py:484
  93.0 12.6 %shard_map.65 = f32[4096,2048]{1,0:T(8,128)} custom-call(f32[4096,2048]{1,0:T(8,128)S(1)} %get-tuple-element.8.refs_0_, f32[2,4,128,2048]{3,2,1,0:T(8,128)S(1)} %get-tuple-element.9.refs_1_, f32[4,128,2048]{2,1,0:T(8,128)S(1)} %get-tuple-element.10.refs_2_), custom_call_target="tpu_custom_call" | custom-call | tf_op jit(solution)/shard_map/pallas_call | solution.py:555

commit v4 on v3

--- a/solution.py
+++ b/solution.py
@@ -50,22 +50,22 @@
     return lax.dot_general(left, right, (((0,), (0,)), ((), ())), preferred_element_type=jnp.float32)
 
 
-def load_right(col, planes, right):
+def load_right(col, planes, right, terms=3):
     depth = col.shape[1]
     for index, plane in enumerate(planes):
         high, low = split_two(col[plane])
-        for part, values in enumerate((high, high, low)):
-            right[pl.ds((3 * index + part) * depth, depth), :] = values
-
-
-def strip_left(rowp, planes, start, height):
+        for part, values in enumerate((high, high, low)[:terms]):
+            right[pl.ds((terms * index + part) * depth, depth), :] = values
+
+
+def strip_left(rowp, planes, start, height, terms=3):
     width = rowp.shape[3]
     half = start // width
     first = pl.multiple_of(start % width, LANES)
     parts = []
     for plane in planes:
         high, low = split_two(rowp[half, plane, :, pl.ds(first, height)])
-        parts += [high, low, high]
+        parts += [high, low, high][:terms]
     return jnp.concatenate(parts, axis=0)
 
 
@@ -142,6 +142,10 @@
     @pl.when(jnp.logical_not(same))
     def _():
         acc[pl.ds(start, height), :] = jnp.zeros((height, width), jnp.float32)
+
+
+def lone_order(row, row_count):
+    return jnp.where((row > 0) & (row < row_count - 1), 0, 2)
 
 
 def gather_kernel(
@@ -332,7 +336,7 @@
     steps = row_count * col_count
     strip = height // col_count
     inner = has_up & has_down
-    behind = jnp.where(inner, 0, 0)
+    behind = 0
     same = (row * height) // patches == (me * width) // patches
     row_line = lax.rem(row * height, patches) // LANES
     col_line = lax.rem(me * width, patches) // LANES
@@ -376,7 +380,7 @@
                 both_sides(far, lambda plane: ring_step(plane, turn, clockwise, hop < limit))
 
         for hop, clockwise in ((hop_cw, True), (hop_ccw, False)):
-            ring_turn(hop, clockwise, 0, 0, col_count)
+            ring_turn(hop, clockwise, 2, 0, col_count)
             ring_turn(hop, clockwise, behind, col_count, steps)
 
         @pl.when((now >= col_count) & (now < 2 * col_count))
@@ -397,7 +401,7 @@
                 down = pl.ds(pl.multiple_of(core * width + block * LANES, LANES), LANES)
                 acc[down, across] = acc[down, across] + jnp.where(corner, line, 0.0)
 
-        def add_planes(begin, orders, strip):
+        def add_planes(begin, orders, strip, terms=3):
             part = now - begin
 
             @pl.when((part >= 0) & (part * strip < height))
@@ -408,21 +412,22 @@
                 def _():
                     for plane in planes:
                         wait_core(plane)
-                    load_right(col, planes, right)
+                    load_right(col, planes, right, terms)
 
                 piece = min(strip, 4 * LANES)
-                used = right.at[pl.ds(0, 3 * len(planes) * col.shape[1]), :]
+                used = right.at[pl.ds(0, terms * len(planes) * col.shape[1]), :]
 
                 @pl.loop(0, strip // piece)
                 def _(block):
                     start = pl.multiple_of(part * strip + block * piece, LANES)
-                    left = strip_left(rowp, planes, start, piece)
+                    left = strip_left(rowp, planes, start, piece, terms)
                     acc[pl.ds(start, piece), :] = acc[pl.ds(start, piece), :] + contract_rows(left, used[...])
 
         if row_count == 4:
             first = jnp.where(inner, 1, 0)
-            add_planes(2 * col_count + lag + behind, (first, first + 1), strip)
-            add_planes(jnp.where(inner, 2 * col_count, 3 * col_count + lag), (jnp.where(inner, 0, 2),), 2 * strip)
+            begin = jnp.where(inner, 2 * col_count + 0, 3 * col_count + lag)
+            add_planes(2 * col_count + lag, (first, first + 1), strip)
+            add_planes(begin, (lone_order(row, row_count),), 2 * strip, 2)
         else:
             order = jnp.clip((now - lag - 2) // col_count - 1, 0, row_count - 2)
             add_planes((order + 1) * col_count + lag + 2, (order,), strip)
@@ -515,7 +520,12 @@
     plane = plane_at(row, row_count - 1, row_count)
     height, width = acc.shape
     strip = stage.shape[1]
+    depth = col.shape[1]
+    shared = row_count == 4
     load_right(col, (plane,), right)
+    if shared:
+        lone = plane_at(row, lone_order(row, row_count), row_count)
+        right[pl.ds(3 * depth, depth), :] = split_two(col[lone])[1]
 
     def copy(index, slot):
         start = pl.multiple_of(index * strip, LANES)
@@ -533,6 +543,8 @@
 
         start = pl.multiple_of(index * strip, LANES)
         left = strip_left(rowp, (plane,), start, strip)
+        if shared:
+            left = jnp.concatenate([left, strip_left(rowp, (lone,), start, strip, 1)], axis=0)
 
         stage[slot] = acc[pl.ds(start, strip), :] + contract_rows(left, right[...])
         copy(index, slot).start()
@@ -559,7 +571,7 @@
         out_specs=pl.BlockSpec(memory_space=pl.ANY),
         scratch_shapes=[
             pltpu.VMEM((slots, strip, width), jnp.float32),
-            pltpu.VMEM((3 * depth, width), jnp.bfloat16),
+            pltpu.VMEM(((4 if row_count == 4 else 3) * depth, width), jnp.bfloat16),
             pltpu.SemaphoreType.DMA((slots,)),
         ],
         compiler_params=pltpu.CompilerParams(vmem_limit_bytes=VMEM_GRANT),

time: 106 us -> 101 us (0.953)
  the two profiles are of different devices: /device:TPU:25 before, /device:TPU:16 now
where the time goes in v4:
time: 101 us
  Pallas kernels  101 us (100%)
    pallas_call x1, Pallas kernels, gather_and_sum(): pl.pallas_call(body, out_shape=(pltpu.VMEM((height, width), jnp.float32),...  87.9 us
    pallas_call x1, Pallas kernels, finish(): pl.pallas_call(body, out_shape=jax.ShapeDtypeStruct((height, width), jnp....  12.8 us

profile of v4, /device:TPU:16, one launch (start us, length us, event | category | flops | bytes accessed | tf_op | source)
XLA Modules:
  0.0 100.7 jit_solution(4921293553419882966)
XLA Ops:
  0.0 87.9 %shard_map.64 = (f32[4096,2048]{1,0:T(8,128)S(1)}, f32[2,4,128,2048]{3,2,1,0:T(8,128)S(1)}, f32[4,128,2048]{2,1,0:T(8,128)S(1)}) custom-call(f32[16,16384]{1,0:T(8,128)} %refs_0_.1, f32[16]{0:T(128)} %refs_1_.1, s32[16]{0:T(128)} %refs_2_.1, f32[4]{0:T(128)} %refs_3_.1, f32[64,128]{1,0:T(8,128)} %bitcast.2, s32[64,128]{1,0:T(8,128)} %bitcast.3), custom_call_target="tpu_custom_call" | custom-call | tf_op jit(solution)/shard_map/pallas_call | solution.py:489
  87.9 12.8 %shard_map.65 = f32[4096,2048]{1,0:T(8,128)} custom-call(f32[4096,2048]{1,0:T(8,128)S(1)} %get-tuple-element.8.refs_0_, f32[2,4,128,2048]{3,2,1,0:T(8,128)S(1)} %get-tuple-element.9.refs_1_, f32[4,128,2048]{2,1,0:T(8,128)S(1)} %get-tuple-element.10.refs_2_), custom_call_target="tpu_custom_call" | custom-call | tf_op jit(solution)/shard_map/pallas_call | solution.py:567
